TPU v7x, 32 devices: a whole 2x2x4 slice. The times are simulated.
32 devices in a mesh: rows: 16 (over z, y, x), sub: 2 (over core).
Axes of the slice: x: 2, y: 2, z: 4, core: 2. Of those that a mesh axis runs over, the one named last changes fastest.
Arguments:
- matrix: float32 [4096, 384], P(('rows', 'sub')), as said below
- grad_out: float32 [4096, 384], P(('rows', 'sub')), as said below
- grad_factor: float32 [384, 384], replicated, may hold values from -6 to 6
Outputs:
- grad_matrix: float32 [4096, 384], P(('rows', 'sub'))
Inputs may be any that keep to these rules, and one draw needn't show every extreme that they name: `matrix`: entries at most of order 1 / sqrt(4096), with a scale that varies by row and by column. `grad_out`: entries of order 0.01.
All inputs are finite; a program needn't handle non-finite values.
Results may differ from a plain program's by a relative error of at most 0.0004.
Values sent between devices are 32-bit elements; how exact they have to be, the bound alone decides.
No kernel may reach another device: no remote copies, remote signals or barrier semaphores. Data moves between devices by JAX's collectives and lax.ppermute only.
A program may use at most 64 MiB of HBM per device.

v0:
```python
import jax
import jax.numpy as jnp
from jax import lax
from jax.sharding import PartitionSpec as P

SECTIONS = 2
shift_frac = 0.02


def full_dot(left, right):
    return jnp.dot(left, right, precision=lax.Precision.HIGHEST, preferred_element_type=jnp.float32)


def inner_gram(left, right):
    return lax.dot_general(
        left,
        right,
        (((0,), (0,)), ((), ())),
        precision=lax.Precision.HIGHEST,
        preferred_element_type=jnp.float32,
    )


def cholesky_adjoint(lower_fac, lower_inv, lower_grad):
    product = full_dot(lower_fac.T, lower_grad)
    phi_part = jnp.tril(product) - 0.5 * jnp.diag(jnp.diag(product))
    sandwich = full_dot(full_dot(lower_inv.T, phi_part), lower_inv)
    return 0.5 * (sandwich + sandwich.T)


def factor_grads(uppers, grad_factor):
    count = len(uppers)
    result = []
    for section_index in range(count):
        middle = grad_factor
        for later in range(section_index + 1, count):
            middle = full_dot(uppers[later].T, middle)
        for earlier in range(section_index - 1, -1, -1):
            middle = full_dot(middle, uppers[earlier].T)
        result.append(middle)
    return result


def summed_gram(partial_value):
    half_rows = lax.psum_scatter(partial_value, "sub", scatter_dimension=0, tiled=True)
    half_rows = lax.psum(half_rows, "rows")
    return lax.all_gather(half_rows, "sub", axis=0, tiled=True)


def per_device(matrix, grad_out, grad_factor):
    width = matrix.shape[1]
    rate = shift_frac / width
    identity = jnp.eye(width, dtype=jnp.float32)
    current = matrix
    saved = []
    for section_index in range(SECTIONS):
        summed = summed_gram(inner_gram(current, current))
        shift_val = rate * jnp.trace(summed)
        lower_fac = jnp.linalg.cholesky(summed + shift_val * identity)
        lower_inv = lax.linalg.triangular_solve(lower_fac, identity, left_side=True, lower=True)
        following = full_dot(current, lower_inv.T)
        saved.append((current, following, lower_fac, lower_inv))
        current = following
    uppers = [item[2].T for item in saved]
    fac_grads = factor_grads(uppers, grad_factor)
    q_grad = grad_out
    for section_index in range(SECTIONS - 1, -1, -1):
        before, after, lower_fac, lower_inv = saved[section_index]
        crossed = lax.psum(inner_gram(after, q_grad), ("rows", "sub"))
        total_grad = fac_grads[section_index] - full_dot(crossed, lower_inv)
        gram_grad = cholesky_adjoint(lower_fac, lower_inv, jnp.tril(total_grad.T))
        gram_grad = gram_grad + rate * jnp.trace(gram_grad) * identity
        q_grad = full_dot(q_grad, lower_inv) + 2.0 * full_dot(before, gram_grad)
    return q_grad


def solution(mesh):
    placed = (P(("rows", "sub"), None), P(("rows", "sub"), None), P())
    return jax.shard_map(
        per_device, mesh=mesh, in_specs=placed, out_specs=P(("rows", "sub"), None), check_vma=False
    )
```

profile of v0, /device:TPU:0, one launch (start us, length us, event | category | flops | bytes accessed | tf_op | source)
XLA Modules:
  0.0 777.9 jit_solution(7228258176599560391)
XLA Ops:
  6.5 2.6 fusion.120
  9.2 11.2 %reduce-scatter.7.cloned.1.call-done = f32[192,384]{1,0:T(8,128)} async-done(((f32[384,384]{1,0:T(8,128)}), f32[192,384]{1,0:T(8,128)}) %reduce-scatter.7.cloned.1.call-update) | async-done | bytes 294928
  20.3 1.9 copy.59
  22.4 113.0 %all-reduce.6.cloned.1.call-done = f32[192,384]{0,1:T(8,128)} async-done(((f32[192,384]{0,1:T(8,128)}), f32[192,384]{0,1:T(8,128)}) %all-reduce.6.cloned.1.call-update) | async-done | bytes 294928 | tf_op jit(solution)/shard_map/psum | solution.py:46
  135.3 1.1 copy.25
  136.5 2.2 all_gather.6
  140.5 11.7 %cholesky.208 = f32[128,128]{1,0:T(8,128)S(1)} custom-call(f32[128,128]{1,0:T(8,128)S(1)} %cholesky.310), custom_call_target="Cholesky" | custom-call | tf_op jit(solution)/shard_map/jit(cholesky)/cholesky | solution.py:59
  152.3 9.8 %custom-call.24 = f32[1,128,128]{1,2,0:T(8,128)S(1)} custom-call(f32[1,128,128]{2,1,0:T(8,128)S(1)} %get-tuple-element.56), custom_call_target="InvertDiagBlocksLowerTriangular" | custom-call | tf_op jit(solution)/shard_map/jit(cholesky)/cholesky | solution.py:59
  162.7 11.7 %cholesky.227 = f32[128,128]{1,0:T(8,128)S(1)} custom-call(f32[128,128]{1,0:T(8,128)S(1)} %cholesky.314), custom_call_target="Cholesky" | custom-call | tf_op jit(solution)/shard_map/jit(cholesky)/cholesky | solution.py:59
  174.5 10.0 %custom-call.25 = f32[1,128,128]{1,2,0:T(8,128)S(1)} custom-call(f32[1,128,128]{2,1,0:T(8,128)S(1)} %get-tuple-element.53), custom_call_target="InvertDiagBlocksLowerTriangular" | custom-call | tf_op jit(solution)/shard_map/jit(cholesky)/cholesky | solution.py:59
  184.9 11.7 %cholesky.246 = f32[128,128]{1,0:T(8,128)S(1)} custom-call(f32[128,128]{1,0:T(8,128)S(1)} %convolution_subtract_fusion.9), custom_call_target="Cholesky" | custom-call | tf_op jit(solution)/shard_map/jit(cholesky)/cholesky | solution.py:59
  200.0 6.0 while.4
  200.7 1.3 bitcast_dynamic-update-slice_fusion.4
  202.7 1.3 bitcast_dynamic-update-slice_fusion.4
  204.7 1.3 bitcast_dynamic-update-slice_fusion.4
  206.0 29.5 %custom-call.26 = f32[3,128,128]{1,2,0:T(8,128)S(1)} custom-call(f32[3,128,128]{2,1,0:T(8,128)S(1)} %get-tuple-element.21), custom_call_target="InvertDiagBlocksLowerTriangular" | custom-call | tf_op jit(solution)/shard_map/triangular_solve/custom-call.2 | solution.py:60
  236.8 0.8 convolution_subtract_fusion.4
  239.2 1.4 fusion.121
  240.7 7.1 reduce-scatter.9.cloned.1.call-done
  247.8 1.9 copy.61
  249.8 112.9 %all-reduce.8.cloned.1.call-done = f32[192,384]{0,1:T(8,128)} async-done(((f32[192,384]{0,1:T(8,128)}), f32[192,384]{0,1:T(8,128)}) %all-reduce.8.cloned.1.call-update) | async-done | bytes 294928 | tf_op jit(solution)/shard_map/psum | solution.py:46
  362.7 1.1 copy.32
  363.8 2.4 all_gather.7
  367.8 1.0 copy.35
  368.8 1.1 fusion.6
  370.0 11.7 %cholesky.261 = f32[128,128]{1,0:T(8,128)S(1)} custom-call(f32[128,128]{1,0:T(8,128)S(1)} %cholesky.318), custom_call_target="Cholesky" | custom-call | tf_op jit(solution)/shard_map/jit(cholesky)/cholesky | solution.py:59
  381.8 9.8 %custom-call.27 = f32[1,128,128]{1,2,0:T(8,128)S(1)} custom-call(f32[1,128,128]{2,1,0:T(8,128)S(1)} %get-tuple-element.49), custom_call_target="InvertDiagBlocksLowerTriangular" | custom-call | tf_op jit(solution)/shard_map/jit(cholesky)/cholesky | solution.py:59
  392.2 11.7 %cholesky.280 = f32[128,128]{1,0:T(8,128)S(1)} custom-call(f32[128,128]{1,0:T(8,128)S(1)} %cholesky.322), custom_call_target="Cholesky" | custom-call | tf_op jit(solution)/shard_map/jit(cholesky)/cholesky | solution.py:59
  405.3 10.2 %custom-call.28 = f32[1,128,128]{1,2,0:T(8,128)S(1)} custom-call(f32[1,128,128]{2,1,0:T(8,128)S(1)} %get-tuple-element.46), custom_call_target="InvertDiagBlocksLowerTriangular" | custom-call | tf_op jit(solution)/shard_map/jit(cholesky)/cholesky | solution.py:59
  416.0 11.7 %cholesky.299 = f32[128,128]{1,0:T(8,128)S(1)} custom-call(f32[128,128]{1,0:T(8,128)S(1)} %convolution_subtract_fusion.8), custom_call_target="Cholesky" | custom-call | tf_op jit(solution)/shard_map/jit(cholesky)/cholesky | solution.py:59
  430.4 0.9 fusion.11
  431.3 8.7 %while.5 = (s32[]{:T(128)}, f32[384,384]{1,0:T(8,128)}, s32[3,2]{0,1:T(2,128)S(1)}, f32[3,128,128]{2,1,0:T(8,128)S(1)}, s32[]{:T(128)}) while((s32[]{:T(128)}, f32[384,384]{1,0:T(8,128)}, s32[3,2]{0,1:T(2,128)S(1)}, f32[3,128,128]{2,1,0:T(8,128)S(1)}, s32[]{:T(128)}) %tuple.65), condition=%wide.while_cond.clone, body=%wide.while_body.clone.sunk | while | flops 2 | bytes 131181 | solution.py:60
  431.9 2.2 bitcast_dynamic-update-slice_fusion.5
  434.8 2.2 bitcast_dynamic-update-slice_fusion.5
  437.8 2.2 bitcast_dynamic-update-slice_fusion.5
  439.9 29.5 %custom-call.29 = f32[3,128,128]{1,2,0:T(8,128)S(1)} custom-call(f32[3,128,128]{2,1,0:T(8,128)S(1)} %get-tuple-element.22), custom_call_target="InvertDiagBlocksLowerTriangular" | custom-call | tf_op jit(solution)/shard_map/triangular_solve/custom-call.2 | solution.py:60
  470.1 1.3 convolution_subtract_fusion.3
  471.5 1.2 fusion.78
  472.7 1.7 convolution_subtract_fusion.2
  474.4 1.2 fusion.76
  475.7 0.8 fusion.115
  476.7 1.5 fusion.122
  478.5 2.1 fusion.38
  480.6 125.3 %all-reduce.10.cloned.1.call-done = f32[384,384]{1,0:T(8,128)} async-done(((f32[384,384]{1,0:T(8,128)}), f32[384,384]{1,0:T(8,128)}) %all-reduce.10.cloned.1.call-update) | async-done | bytes 589840 | tf_op jit(solution)/shard_map/psum | solution.py:69
  605.9 2.5 fusion
  608.4 1.5 fusion.34
  609.9 1.0 copy.40
  611.0 3.4 gather_fusion
  614.4 3.3 fusion.21
  617.7 1.3 fusion.114
  619.0 1.0 copy.41
  620.0 1.7 select_reduce_fusion.1
  622.4 1.8 convolution_multiply_fusion.1
  624.2 1.1 fusion.3
  625.3 1.4 fusion.123
  626.8 1.3 convolution_bitcast_fusion
  628.1 127.6 %all-reduce.12.cloned.1.call-done = f32[384,384]{1,0:T(8,128)} async-done(((f32[384,384]{1,0:T(8,128)}), f32[384,384]{1,0:T(8,128)}) %all-reduce.12.cloned.1.call-update) | async-done | bytes 589840 | tf_op jit(solution)/shard_map/psum | solution.py:69
  755.7 2.4 fusion.1
  758.1 1.5 fusion.36
  759.8 3.7 gather_fusion.1
  763.5 2.1 fusion.14
  765.6 1.3 fusion.116
  768.6 0.8 fusion.2
  769.5 1.3 convolution_add_fusion
  (103 shorter events, 17.5 us)
Async XLA Ops:
  6.5 471.9 %copy-start = (f32[384,384]{1,0:T(8,128)S(1)}, f32[384,384]{1,0:T(8,128)}, u32[]{:S(2)}) copy-start(f32[384,384]{1,0:T(8,128)} %param.8) | copy-start | bytes 1769476
  6.5 13.8 %reduce-scatter.7.cloned.1.call-start = ((), (), s32[]{:S(2)}) async-start(), calls=%async_computation.6 | async-start | bytes 884736
  9.1 126.2 %all-reduce.6.cloned.1.call-start = ((), (), s32[]{:S(2)}) async-start(), calls=%async_computation.2 | async-start | bytes 786432 | tf_op jit(solution)/shard_map/psum | solution.py:46
  22.2 225.6 %reduce-scatter.9.cloned.1.call-start = ((), (), s32[]{:S(2)}) async-start(), calls=%async_computation.7 | async-start | bytes 884736
  22.3 214.5 %copy-start.1 = (f32[384,384]{0,1:T(8,128)}, f32[384,384]{0,1:T(8,128)S(1)}, u32[]{:S(2)}) copy-start(f32[384,384]{0,1:T(8,128)S(1)} %fusion.26) | copy-start | bytes 1769476
  237.6 0.9 copy-start.6
  240.7 122.0 %all-reduce.8.cloned.1.call-start = ((), (), s32[]{:S(2)}) async-start(), calls=%async_computation.3 | async-start | bytes 786432 | tf_op jit(solution)/shard_map/psum | solution.py:46
  249.7 356.1 %all-reduce.10.cloned.1.call-start = ((), (), s32[]{:S(2)}) async-start(), calls=%async_computation.4 | async-start | bytes 1179648 | tf_op jit(solution)/shard_map/psum | solution.py:69
  370.0 11.7 %copy-start.10 = (f32[384,384]{1,0:T(8,128)}, f32[384,384]{1,0:T(8,128)S(1)}, u32[]{:S(2)}) copy-start(f32[384,384]{1,0:T(8,128)S(1)} %fusion.6) | copy-start | bytes 1769476
  381.7 9.9 %copy-start.11 = (f32[384,384]{1,0:T(8,128)S(1)}, f32[384,384]{1,0:T(8,128)}, u32[]{:S(2)}) copy-start(f32[384,384]{1,0:T(8,128)} %copy-done.10) | copy-start | bytes 1769476
  430.4 39.1 %copy-start.2 = (f32[384,384]{0,1:T(8,128)S(1)}, f32[384,384]{0,1:T(8,128)}, u32[]{:S(2)}) copy-start(f32[384,384]{0,1:T(8,128)} %copy-done.1) | copy-start | bytes 1769476
  469.5 0.7 copy-start.14
  475.7 130.2 %copy-start.3 = (f32[128,384]{1,0:T(8,128)}, f32[128,384]{1,0:T(8,128)S(1)}, u32[]{:S(2)}) copy-start(f32[128,384]{1,0:T(8,128)S(1)} %fusion.76) | copy-start | bytes 589828
  475.7 1.0 copy-start.12
  478.2 277.5 %all-reduce.12.cloned.1.call-start = ((), (), s32[]{:S(2)}) async-start(), calls=%async_computation.5 | async-start | bytes 1179648 | tf_op jit(solution)/shard_map/psum | solution.py:69
  614.4 3.3 copy-start.4
  622.3 1.8 copy-start.5
  622.3 1.8 copy-start.13
  625.3 1.5 copy-start.8
  767.1 1.4 copy-start.7
  768.5 0.9 copy-start.9
Sparse Core Ops, SparseCore 0:
  9.6 10.6 reduce-scatter.6
  25.5 109.7 all-reduce.5
  240.8 6.9 reduce-scatter.8
  252.9 109.7 all-reduce.7
  478.4 127.4 all-reduce.9
  626.9 128.7 all-reduce.11
where the time goes:
time: 788 us; the launch traced here: 778 us
  waiting for transfers between devices  497 us (63%)
  other arithmetic  179 us (23%)
  matrix products  43.1 us (5%)
  local copies, waits for them, and re-layouts  33.2 us (4%)
  between operations  20.5 us (3%)
    psum x2, waiting for transfers between devices, per_device(): crossed = lax.psum(inner_gram(after, q_grad), ('rows', 'sub'))  253 us
    psum x2, waiting for transfers between devices, summed_gram(): half_rows = lax.psum(half_rows, 'rows')  226 us
    another operation x21, other arithmetic, per_device(): lower_fac = jnp.linalg.cholesky(summed + shift_val * identity)  114 us
    another operation x5, other arithmetic, per_device(): lax.linalg.triangular_solve(lower_fac, identity, left_side=True, lower=True)  59.9 us
    dot_general x16, matrix products, full_dot(): jnp.dot(left, right, precision=lax.Precision.HIGHEST, preferred_element_t...  25.7 us
    unnamed x8, waiting for transfers between devices  18.4 us
  transfers between devices with their start and end apart: 6, of which 6 were waited for; matrix products, arithmetic and copies ran while one was open for 0% of the time, Pallas kernels for 0%

commit v1 on v0

--- a/solution.py
+++ b/solution.py
@@ -66,7 +66,7 @@
     q_grad = grad_out
     for section_index in range(SECTIONS - 1, -1, -1):
         before, after, lower_fac, lower_inv = saved[section_index]
-        crossed = lax.psum(inner_gram(after, q_grad), ("rows", "sub"))
+        crossed = lax.psum(lax.psum(inner_gram(after, q_grad), "sub"), "rows")
         total_grad = fac_grads[section_index] - full_dot(crossed, lower_inv)
         gram_grad = cholesky_adjoint(lower_fac, lower_inv, jnp.tril(total_grad.T))
         gram_grad = gram_grad + rate * jnp.trace(gram_grad) * identity

time: 788 us -> 800 us (1.015)
  waiting for transfers between devices: 497 us -> 509 us
    psum x2 -> x4, waiting for transfers between devices: 253 us -> 265 us  [per_device(): crossed = lax.psum(lax.psum(inner_gram(after, q_grad), 'sub'), 'rows')]
    unnamed x8 -> x10, waiting for transfers between devices: 18.4 us -> 18.4 us
  transfers between devices with their start and end apart: 6 -> 8, of which waited for: 6 -> 8; matrix products, arithmetic and copies ran while one was open for 0% -> 0% of each run, Pallas kernels for 0% -> 0%
where the time goes in v1:
time: 800 us; the launch traced here: 789 us
  waiting for transfers between devices  509 us (64%)
  other arithmetic  179 us (22%)
  matrix products  43 us (5%)
  local copies, waits for them, and re-layouts  32.9 us (4%)
  between operations  20.4 us (3%)
    psum x4, waiting for transfers between devices, per_device(): crossed = lax.psum(lax.psum(inner_gram(after, q_grad), 'sub'), 'rows')  265 us
    psum x2, waiting for transfers between devices, summed_gram(): half_rows = lax.psum(half_rows, 'rows')  226 us
    another operation x21, other arithmetic, per_device(): lower_fac = jnp.linalg.cholesky(summed + shift_val * identity)  114 us
    another operation x5, other arithmetic, per_device(): lax.linalg.triangular_solve(lower_fac, identity, left_side=True, lower=True)  59.9 us
    dot_general x16, matrix products, full_dot(): jnp.dot(left, right, precision=lax.Precision.HIGHEST, preferred_element_t...  25.6 us
    unnamed x10, waiting for transfers between devices  18.4 us
  transfers between devices with their start and end apart: 8, of which 8 were waited for; matrix products, arithmetic and copies ran while one was open for 0% of the time, Pallas kernels for 0%

profile of v1, /device:TPU:0, one launch (start us, length us, event | category | flops | bytes accessed | tf_op | source)
XLA Modules:
  0.0 789.3 jit_solution(16242251197540875857)
XLA Ops:
  6.5 2.6 fusion.120
  9.2 11.2 %reduce-scatter.7.cloned.1.call-done = f32[192,384]{1,0:T(8,128)} async-done(((f32[384,384]{1,0:T(8,128)}), f32[192,384]{1,0:T(8,128)}) %reduce-scatter.7.cloned.1.call-update) | async-done | bytes 294928
  20.3 1.9 copy.59
  22.4 113.0 %all-reduce.8.cloned.1.call-done = f32[192,384]{0,1:T(8,128)} async-done(((f32[192,384]{0,1:T(8,128)}), f32[192,384]{0,1:T(8,128)}) %all-reduce.8.cloned.1.call-update) | async-done | bytes 294928 | tf_op jit(solution)/shard_map/psum | solution.py:46
  135.3 1.1 copy.25
  136.5 2.2 all_gather.6
  140.5 11.7 %cholesky.208 = f32[128,128]{1,0:T(8,128)S(1)} custom-call(f32[128,128]{1,0:T(8,128)S(1)} %cholesky.310), custom_call_target="Cholesky" | custom-call | tf_op jit(solution)/shard_map/jit(cholesky)/cholesky | solution.py:59
  152.3 9.8 %custom-call.24 = f32[1,128,128]{1,2,0:T(8,128)S(1)} custom-call(f32[1,128,128]{2,1,0:T(8,128)S(1)} %get-tuple-element.56), custom_call_target="InvertDiagBlocksLowerTriangular" | custom-call | tf_op jit(solution)/shard_map/jit(cholesky)/cholesky | solution.py:59
  162.7 11.7 %cholesky.227 = f32[128,128]{1,0:T(8,128)S(1)} custom-call(f32[128,128]{1,0:T(8,128)S(1)} %cholesky.314), custom_call_target="Cholesky" | custom-call | tf_op jit(solution)/shard_map/jit(cholesky)/cholesky | solution.py:59
  174.5 10.2 %custom-call.25 = f32[1,128,128]{1,2,0:T(8,128)S(1)} custom-call(f32[1,128,128]{2,1,0:T(8,128)S(1)} %get-tuple-element.53), custom_call_target="InvertDiagBlocksLowerTriangular" | custom-call | tf_op jit(solution)/shard_map/jit(cholesky)/cholesky | solution.py:59
  185.2 11.7 %cholesky.246 = f32[128,128]{1,0:T(8,128)S(1)} custom-call(f32[128,128]{1,0:T(8,128)S(1)} %convolution_subtract_fusion.9), custom_call_target="Cholesky" | custom-call | tf_op jit(solution)/shard_map/jit(cholesky)/cholesky | solution.py:59
  200.3 6.0 while.4
  201.0 1.3 bitcast_dynamic-update-slice_fusion.4
  203.0 1.3 bitcast_dynamic-update-slice_fusion.4
  205.0 1.3 bitcast_dynamic-update-slice_fusion.4
  206.3 29.5 %custom-call.26 = f32[3,128,128]{1,2,0:T(8,128)S(1)} custom-call(f32[3,128,128]{2,1,0:T(8,128)S(1)} %get-tuple-element.21), custom_call_target="InvertDiagBlocksLowerTriangular" | custom-call | tf_op jit(solution)/shard_map/triangular_solve/custom-call.2 | solution.py:60
  239.5 1.4 fusion.121
  241.0 7.1 reduce-scatter.9.cloned.1.call-done
  248.1 1.9 copy.61
  250.1 112.9 %all-reduce.10.cloned.1.call-done = f32[192,384]{0,1:T(8,128)} async-done(((f32[192,384]{0,1:T(8,128)}), f32[192,384]{0,1:T(8,128)}) %all-reduce.10.cloned.1.call-update) | async-done | bytes 294928 | tf_op jit(solution)/shard_map/psum | solution.py:46
  362.9 1.1 copy.32
  364.1 2.4 all_gather.7
  368.0 1.0 copy.35
  369.0 1.1 fusion.6
  370.2 11.7 %cholesky.261 = f32[128,128]{1,0:T(8,128)S(1)} custom-call(f32[128,128]{1,0:T(8,128)S(1)} %cholesky.318), custom_call_target="Cholesky" | custom-call | tf_op jit(solution)/shard_map/jit(cholesky)/cholesky | solution.py:59
  382.0 9.8 %custom-call.27 = f32[1,128,128]{1,2,0:T(8,128)S(1)} custom-call(f32[1,128,128]{2,1,0:T(8,128)S(1)} %get-tuple-element.49), custom_call_target="InvertDiagBlocksLowerTriangular" | custom-call | tf_op jit(solution)/shard_map/jit(cholesky)/cholesky | solution.py:59
  392.4 11.7 %cholesky.280 = f32[128,128]{1,0:T(8,128)S(1)} custom-call(f32[128,128]{1,0:T(8,128)S(1)} %cholesky.322), custom_call_target="Cholesky" | custom-call | tf_op jit(solution)/shard_map/jit(cholesky)/cholesky | solution.py:59
  405.4 10.0 %custom-call.28 = f32[1,128,128]{1,2,0:T(8,128)S(1)} custom-call(f32[1,128,128]{2,1,0:T(8,128)S(1)} %get-tuple-element.46), custom_call_target="InvertDiagBlocksLowerTriangular" | custom-call | tf_op jit(solution)/shard_map/jit(cholesky)/cholesky | solution.py:59
  415.9 11.7 %cholesky.299 = f32[128,128]{1,0:T(8,128)S(1)} custom-call(f32[128,128]{1,0:T(8,128)S(1)} %convolution_subtract_fusion.8), custom_call_target="Cholesky" | custom-call | tf_op jit(solution)/shard_map/jit(cholesky)/cholesky | solution.py:59
  430.3 0.9 fusion.11
  431.2 8.7 %while.5 = (s32[]{:T(128)}, f32[384,384]{1,0:T(8,128)}, s32[3,2]{0,1:T(2,128)S(1)}, f32[3,128,128]{2,1,0:T(8,128)S(1)}, s32[]{:T(128)}) while((s32[]{:T(128)}, f32[384,384]{1,0:T(8,128)}, s32[3,2]{0,1:T(2,128)S(1)}, f32[3,128,128]{2,1,0:T(8,128)S(1)}, s32[]{:T(128)}) %tuple.69), condition=%wide.while_cond.clone, body=%wide.while_body.clone.sunk | while | flops 2 | bytes 131181 | solution.py:60
  431.9 2.2 bitcast_dynamic-update-slice_fusion.5
  434.8 2.2 bitcast_dynamic-update-slice_fusion.5
  437.7 2.2 bitcast_dynamic-update-slice_fusion.5
  439.9 29.5 %custom-call.29 = f32[3,128,128]{1,2,0:T(8,128)S(1)} custom-call(f32[3,128,128]{2,1,0:T(8,128)S(1)} %get-tuple-element.22), custom_call_target="InvertDiagBlocksLowerTriangular" | custom-call | tf_op jit(solution)/shard_map/triangular_solve/custom-call.2 | solution.py:60
  470.1 1.3 convolution_subtract_fusion.3
  471.4 1.2 fusion.78
  472.6 1.7 convolution_subtract_fusion.2
  474.4 1.2 fusion.76
  475.6 0.8 fusion.115
  476.6 1.5 fusion.122
  478.2 17.8 %all-reduce.12.cloned.1.call-done = f32[384,384]{1,0:T(8,128)} async-done(((f32[384,384]{1,0:T(8,128)}), f32[384,384]{1,0:T(8,128)}) %all-reduce.12.cloned.1.call-update) | async-done | bytes 589840 | tf_op jit(solution)/shard_map/psum | solution.py:69
  496.5 2.1 fusion.38
  498.6 113.8 %all-reduce.14.cloned.1.call-done = f32[384,384]{1,0:T(8,128)} async-done(((f32[384,384]{1,0:T(8,128)}), f32[384,384]{1,0:T(8,128)}) %all-reduce.14.cloned.1.call-update) | async-done | bytes 589840 | tf_op jit(solution)/shard_map/psum | solution.py:69
  612.4 2.5 fusion
  615.0 1.5 fusion.34
  616.5 1.0 copy.40
  617.5 3.4 gather_fusion
  621.0 3.3 fusion.21
  624.2 1.3 fusion.114
  625.5 1.0 copy.41
  626.6 1.7 select_reduce_fusion.1
  628.9 1.8 convolution_multiply_fusion.1
  630.7 1.1 fusion.3
  631.9 1.4 fusion.123
  633.6 17.6 %all-reduce.16.cloned.1.call-done = f32[384,384]{1,0:T(8,128)} async-done(((f32[384,384]{1,0:T(8,128)}), f32[384,384]{1,0:T(8,128)}) %all-reduce.16.cloned.1.call-update) | async-done | bytes 589840 | tf_op jit(solution)/shard_map/psum | solution.py:69
  651.2 1.3 convolution_bitcast_fusion
  652.5 115.3 %all-reduce.18.cloned.1.call-done = f32[384,384]{1,0:T(8,128)} async-done(((f32[384,384]{1,0:T(8,128)}), f32[384,384]{1,0:T(8,128)}) %all-reduce.18.cloned.1.call-update) | async-done | bytes 589840 | tf_op jit(solution)/shard_map/psum | solution.py:69
  767.8 2.4 fusion.1
  770.1 1.5 fusion.36
  771.9 3.4 gather_fusion.1
  775.3 2.1 fusion.14
  777.4 1.3 fusion.116
  781.0 1.3 convolution_add_fusion
  (101 shorter events, 19.4 us)
Async XLA Ops:
  6.5 490.0 %copy-start = (f32[384,384]{1,0:T(8,128)S(1)}, f32[384,384]{1,0:T(8,128)}, u32[]{:S(2)}) copy-start(f32[384,384]{1,0:T(8,128)} %param.8) | copy-start | bytes 1769476
  6.5 13.8 %reduce-scatter.7.cloned.1.call-start = ((), (), s32[]{:S(2)}) async-start(), calls=%async_computation.8 | async-start | bytes 884736
  9.1 126.2 %all-reduce.8.cloned.1.call-start = ((), (), s32[]{:S(2)}) async-start(), calls=%async_computation.2 | async-start | bytes 786432 | tf_op jit(solution)/shard_map/psum | solution.py:46
  22.2 225.9 %reduce-scatter.9.cloned.1.call-start = ((), (), s32[]{:S(2)}) async-start(), calls=%async_computation.9 | async-start | bytes 884736
  22.3 214.8 %copy-start.1 = (f32[384,384]{0,1:T(8,128)}, f32[384,384]{0,1:T(8,128)S(1)}, u32[]{:S(2)}) copy-start(f32[384,384]{0,1:T(8,128)S(1)} %fusion.26) | copy-start | bytes 1769476
  237.9 0.9 copy-start.6
  241.0 122.0 %all-reduce.10.cloned.1.call-start = ((), (), s32[]{:S(2)}) async-start(), calls=%async_computation.3 | async-start | bytes 786432 | tf_op jit(solution)/shard_map/psum | solution.py:46
  250.0 246.0 %all-reduce.12.cloned.1.call-start = ((), (), s32[]{:S(2)}) async-start(), calls=%async_computation.4 | async-start | bytes 1179648 | tf_op jit(solution)/shard_map/psum | solution.py:69
  430.3 39.1 %copy-start.2 = (f32[384,384]{0,1:T(8,128)S(1)}, f32[384,384]{0,1:T(8,128)}, u32[]{:S(2)}) copy-start(f32[384,384]{0,1:T(8,128)} %copy-done.1) | copy-start | bytes 1769476
  469.4 0.7 copy-start.10
  475.6 136.8 %copy-start.3 = (f32[128,384]{1,0:T(8,128)}, f32[128,384]{1,0:T(8,128)S(1)}, u32[]{:S(2)}) copy-start(f32[128,384]{1,0:T(8,128)S(1)} %fusion.76) | copy-start | bytes 589828
  475.6 1.0 copy-start.8
  478.1 134.3 %all-reduce.14.cloned.1.call-start = ((), (), s32[]{:S(2)}) async-start(), calls=%async_computation.5 | async-start | bytes 1179648 | tf_op jit(solution)/shard_map/psum | solution.py:69
  496.0 155.2 %all-reduce.16.cloned.1.call-start = ((), (), s32[]{:S(2)}) async-start(), calls=%async_computation.6 | async-start | bytes 1179648 | tf_op jit(solution)/shard_map/psum | solution.py:69
  620.9 3.3 copy-start.4
  628.9 1.8 copy-start.5
  628.9 1.8 copy-start.9
  633.3 134.4 %all-reduce.18.cloned.1.call-start = ((), (), s32[]{:S(2)}) async-start(), calls=%async_computation.7 | async-start | bytes 1179648 | tf_op jit(solution)/shard_map/psum | solution.py:69
  778.9 1.3 copy-start.7
Sparse Core Ops, SparseCore 0:
  9.6 10.6 reduce-scatter.6
  25.5 109.7 all-reduce.7
  241.1 6.9 reduce-scatter.8
  253.1 109.7 all-reduce.9
  478.2 17.7 all-reduce.11
  501.2 111.1 all-reduce.13
  633.5 17.6 all-reduce.15
  656.5 111.2 all-reduce.17
